TPU v7x, 512 devices: a whole 4x8x8 slice. The times are simulated.
512 devices in a mesh: dp: 16 (over z, y_lo), comp: 32 (over y_hi, x, core).
Axes of the slice: x: 4, y: 8 (y_hi: 4, y_lo: 2; y = y_hi * 2 + y_lo), z: 8, core: 2. Of those that a mesh axis runs over, the one named last changes fastest.
Arguments:
- vectors: bfloat16 [2048, 256], P('dp'), may hold values from -8 to 8
- centers: float32 [512, 256], P('comp'), may hold values from -1.5 to 1.5
- factors: bfloat16 [512, 256, 256], P('comp', 'dp'), may hold values from -1 to 9.065873, as said below
- mixing: float32 [512], P('comp'), may hold values from 0.0005859375 to 0.005859375
Outputs:
- new_factors: float32 [512, 256, 256], P('comp', 'dp')
- new_means: float32 [512, 256], P('comp')
- new_weights: float32 [512], P('comp')
- evidence: float32 [2048], P('dp')
Inputs may be any that keep to these rules, and one draw needn't show every extreme that they name: `factors`: each component's 256 x 256 factor is lower triangular with a positive diagonal.
All inputs are finite; a program needn't handle non-finite values.
Results may differ from a plain program's by a relative error of at most 0.0003.
Values may be sent and summed in bfloat16 or wider, within the bound.
No kernel may reach another device: no remote copies, remote signals or barrier semaphores. Data moves between devices by JAX's collectives and lax.ppermute only.
A program may use at most 64 MiB of HBM per device.

v0:
```python
import math
import jax
import jax.numpy as jnp
from jax import lax
from jax.sharding import PartitionSpec as P

anneal = 1.0
step_weight = 0.5
ridge_term = 0.01
normal_offset = 0.9189385332046727
exact_mode = lax.Precision.HIGHEST


def sent_to_all(shard, axis):
    copies = jnp.broadcast_to(shard, (lax.axis_size(axis), *shard.shape))
    return lax.all_to_all(copies, axis, split_axis=0, concat_axis=0, tiled=True)


def of_everyone(shard, axis):
    everything = sent_to_all(shard, axis)
    return jnp.max(everything, axis=0)


def taken_together(shard, axis):
    return sent_to_all(shard, axis).sum(axis=0)


def in_order(tiles, dim):
    lengths = list(tiles.shape[1:])
    lengths[dim] *= tiles.shape[0]
    return jnp.moveaxis(tiles, 0, dim).reshape(lengths)


def gather_directly(shard, axis, dim):
    tiles = sent_to_all(shard, axis)
    return in_order(tiles, dim)


def in_blocks(shard, dim, peers):
    lengths = shard.shape
    tiles = shard.reshape(*lengths[:dim], peers, lengths[dim] // peers, *lengths[dim + 1 :])
    return jnp.moveaxis(tiles, dim, 0)


def summed_on_arrival(shard, axis, dim):
    tiles = in_blocks(shard, dim, lax.axis_size(axis))
    arrived = lax.all_to_all(tiles, axis, split_axis=0, concat_axis=0, tiled=True)
    return arrived.sum(axis=0)


def normalize(density, mixing, features):
    scores = anneal * (density + jnp.log(mixing)[:, None] - features * normal_offset)
    row_max = jnp.max(scores, axis=0)
    joined_max = of_everyone(row_max, "comp")
    joined_total = taken_together(jnp.sum(jnp.exp(scores - joined_max[None, :]), axis=0), "comp")
    shares = jnp.exp(scores - joined_max[None, :]) / joined_total[None, :]
    evidence = (joined_max + jnp.log(joined_total)) / anneal
    return (shares, evidence)


def refactor(pieces):
    scaled, moment_part = pieces
    identity = jnp.eye(scaled.shape[-1], dtype=jnp.float32)
    inverse = lax.linalg.triangular_solve(scaled, identity, left_side=True, lower=True)
    covariance = (
        jnp.dot(inverse, inverse.T, precision=exact_mode) + moment_part + ridge_term * identity
    )
    cholesky_factor = jnp.linalg.cholesky(covariance)
    return lax.linalg.triangular_solve(cholesky_factor, identity, left_side=True, lower=True)


def local(vectors, centers, factors, mixing):
    comp_count, row_count, features = factors.shape
    groups = lax.axis_size("dp")
    owned_count = comp_count // groups
    position = lax.axis_index("dp")
    row_start = position * row_count
    everyone = gather_directly(vectors, "dp", 0)
    vector_total = everyone.shape[0]
    block_rows = math.gcd(vector_total, 512)
    block_count = vector_total // block_rows
    shifted = jnp.einsum("krd,kd->kr", factors.astype(jnp.float32), centers, precision=exact_mode)
    diag_block = lax.dynamic_slice_in_dim(factors, row_start, row_count, 2).astype(jnp.float32)
    log_diag = jnp.sum(jnp.log(jnp.diagonal(diag_block, axis1=1, axis2=2)), axis=1)
    flattened = factors.reshape(comp_count * row_count, features)
    vector_blocks = everyone.reshape(block_count, block_rows, features)

    def density_block(vector_block):
        whitened = lax.dot_general(
            flattened, vector_block, (((1,), (1,)), ((), ())), preferred_element_type=jnp.float32
        )
        whitened = whitened.reshape(comp_count, row_count, -1) - shifted[:, :, None]
        return log_diag[:, None] - 0.5 * jnp.sum(whitened * whitened, axis=1)

    partial_density = (
        lax.map(density_block, vector_blocks).transpose(1, 0, 2).reshape(comp_count, vector_total)
    )
    density = summed_on_arrival(partial_density, "dp", 1)
    shares_local, evidence = normalize(density, mixing, features)
    shares_all = gather_directly(shares_local, "dp", 1)
    share_blocks = shares_all.reshape(comp_count, block_count, block_rows).transpose(1, 0, 2)

    def accumulate(running, inputs):
        first_sum, gram_sum = running
        vector_block, share_block = inputs
        wide_block = vector_block.astype(jnp.float32)
        first_sum = first_sum + jnp.dot(share_block, wide_block, precision=exact_mode)
        own_share = lax.dynamic_slice_in_dim(share_block, position * owned_count, owned_count, 0)
        weighted = own_share[:, None, :] * wide_block.T[None]
        weighted = weighted.reshape(owned_count * features, -1)
        gram_term = jnp.dot(weighted, wide_block, precision=exact_mode)
        return ((first_sum, gram_sum + gram_term), None)

    gram_start = jnp.zeros((owned_count * features, features), jnp.float32)
    first_start = jnp.zeros((comp_count, features), jnp.float32)
    (first_moment, gram_sum), unused = lax.scan(
        accumulate, (first_start, gram_start), (vector_blocks, share_blocks)
    )
    counts = jnp.sum(shares_all, axis=1)
    kept_share = (1.0 - step_weight) * mixing
    new_weights = kept_share + step_weight * counts / vector_total
    new_means = (
        kept_share[:, None] * centers + step_weight * first_moment / vector_total
    ) / new_weights[:, None]
    retained = kept_share / new_weights
    own_start = position * owned_count
    kept_own = lax.dynamic_slice_in_dim(kept_share, own_start, owned_count, 0)
    weight_own = lax.dynamic_slice_in_dim(new_weights, own_start, owned_count, 0)
    retained_own = lax.dynamic_slice_in_dim(retained, own_start, owned_count, 0)
    center_own = lax.dynamic_slice_in_dim(centers, own_start, owned_count, 0)
    mean_own = lax.dynamic_slice_in_dim(new_means, own_start, owned_count, 0)
    gram_own = gram_sum.reshape(owned_count, features, features)
    moment_part = (
        kept_own[:, None, None] * center_own[:, :, None] * center_own[:, None, :]
        + step_weight * gram_own / vector_total
    ) / weight_own[:, None, None] - mean_own[:, :, None] * mean_own[:, None, :]
    whole_factors = lax.all_to_all(
        factors.reshape(groups, owned_count, row_count, features),
        "dp",
        split_axis=0,
        concat_axis=2,
        tiled=True,
    )
    scaled = whole_factors[0].astype(jnp.float32) * lax.rsqrt(retained_own)[:, None, None]
    refreshed = lax.map(refactor, (scaled, moment_part))
    new_factors = lax.all_to_all(
        refreshed[None], "dp", split_axis=2, concat_axis=0, tiled=True
    ).reshape(comp_count, row_count, features)
    return (new_factors, new_means, new_weights, evidence)


def solution(mesh):
    return jax.shard_map(
        local,
        mesh=mesh,
        in_specs=(P("dp", None), P("comp", None), P("comp", "dp", None), P("comp")),
        out_specs=(P("comp", "dp", None), P("comp", None), P("comp"), P("dp")),
        check_vma=False,
    )
```

profile of v0, /device:TPU:8, one launch (start us, length us, event | category | flops | bytes accessed | tf_op | source)
XLA Modules:
  0.0 226.2 jit_solution(829906853297270123)
XLA Ops:
  0.6 1.9 broadcast_in_dim.32
  2.6 11.8 %all-to-all-start.1 = ((bf16[16,128,256]{2,1,0:T(8,128)(2,1)}), bf16[16,128,256]{2,1,0:T(8,128)(2,1)S(1)}, u32[]{:S(2)}, u32[]{:S(2)}) async-start(bf16[16,128,256]{2,1,0:T(8,128)(2,1)} %broadcast_in_dim.32), calls=%async_computation.1 | async-start | bytes 2097152 | tf_op jit(solution)/shard_map/all_to_all | solution.py:16
  14.4 0.9 constant_dynamic-slice_fusion.5
  15.5 0.6 gather_fusion
  16.2 1.1 fusion.33
  17.3 24.4 %all-to-all-done.1 = bf16[16,128,256]{2,1,0:T(8,128)(2,1)S(1)} async-done(((bf16[16,128,256]{2,1,0:T(8,128)(2,1)}), bf16[16,128,256]{2,1,0:T(8,128)(2,1)S(1)}, u32[]{:S(2)}, u32[]{:S(2)}) %all-to-all-start.1) | async-done | bytes 1048608 | tf_op jit(solution)/shard_map/all_to_all | solution.py:16
  41.7 5.2 %while.34 = (s32[]{:T(128)}, f32[4,16,512]{2,1,0:T(8,128)S(1)}, f32[16]{0:T(128)S(1)}, bf16[4,512,256]{2,1,0:T(8,128)(2,1)S(1)}, bf16[256,256]{1,0:T(8,128)(2,1)}, /*index=5*/f32[16,16]{1,0:T(8,128)S(1)}, s32[]{:T(128)}) while((s32[]{:T(128)}, f32[4,16,512]{2,1,0:T(8,128)S(1)}, f32[16]{0:T(128)S(1)}, bf16[4,512,256]{2,1,0:T(8,128)(2,1)S(1)}, ...), condition=%wide.region_3.4_spmd, body=%wide.region_1.3_spmd.sunk | while | flops 67510272 | bytes 500309 | solution.py:96
  41.7 1.2 multiply_reduce_fusion.2
  43.0 1.2 multiply_reduce_fusion.2
  44.3 1.2 multiply_reduce_fusion.2
  45.6 1.2 multiply_reduce_fusion.2
  47.0 0.7 copy.58
  47.7 4.5 %all-to-all-start.2 = ((f32[16,16,128]{2,1,0:T(8,128)}), f32[16,16,128]{2,1,0:T(8,128)S(1)}, u32[]{:S(2)}, u32[]{:S(2)}) async-start(f32[16,16,128]{2,1,0:T(8,128)} %copy.58), calls=%async_computation.2 | async-start | bytes 262144 | tf_op jit(solution)/shard_map/all_to_all | solution.py:47
  52.2 8.5 %all-to-all-done.2 = f32[16,16,128]{2,1,0:T(8,128)S(1)} async-done(((f32[16,16,128]{2,1,0:T(8,128)}), f32[16,16,128]{2,1,0:T(8,128)S(1)}, u32[]{:S(2)}, u32[]{:S(2)}) %all-to-all-start.2) | async-done | bytes 131104 | tf_op jit(solution)/shard_map/all_to_all | solution.py:47
  60.8 18.6 %all_to_all.45 = f32[32,1,128]{2,1,0:T(1,128)S(1)} all-to-all(f32[32,1,128]{2,1,0:T(1,128)S(1)} %broadcast_in_dim.33), channel_id=1, replica_groups=mesh['dp'=16,'comp'=32] {'comp'}, dimensions={0} | all-to-all | bytes 32768 | tf_op jit(solution)/shard_map/all_to_all | solution.py:16
  79.6 12.8 %all_to_all.46 = f32[32,1,128]{2,1,0:T(1,128)S(1)} all-to-all(f32[32,1,128]{2,1,0:T(1,128)S(1)} %broadcast_in_dim.34), channel_id=1, replica_groups=mesh['dp'=16,'comp'=32] {'comp'}, dimensions={0} | all-to-all | bytes 32768 | tf_op jit(solution)/shard_map/all_to_all | solution.py:16
  92.4 0.7 broadcast_in_dim.35
  93.1 4.0 %all-to-all-start.5 = ((f32[16,16,128]{2,1,0:T(8,128)}), f32[16,16,128]{2,1,0:T(8,128)S(1)}, u32[]{:S(2)}, u32[]{:S(2)}) async-start(f32[16,16,128]{2,1,0:T(8,128)} %broadcast_in_dim.35), calls=%async_computation.5 | async-start | bytes 262144 | tf_op jit(solution)/shard_map/all_to_all | solution.py:16
  97.2 8.5 %all-to-all-done.5 = f32[16,16,128]{2,1,0:T(8,128)S(1)} async-done(((f32[16,16,128]{2,1,0:T(8,128)}), f32[16,16,128]{2,1,0:T(8,128)S(1)}, u32[]{:S(2)}, u32[]{:S(2)}) %all-to-all-start.5) | async-done | bytes 131104 | tf_op jit(solution)/shard_map/all_to_all | solution.py:16
  105.7 4.3 %all-to-all-start = ((bf16[16,1,16,256]{3,2,1,0:T(8,128)(2,1)}), bf16[16,1,16,256]{3,2,1,0:T(8,128)(2,1)S(1)}, u32[]{:S(2)}, u32[]{:S(2)}) async-start(bf16[16,1,16,256]{3,2,1,0:T(8,128)(2,1)} %bitcast.4), calls=%async_computation | async-start | bytes 262144 | tf_op jit(solution)/shard_map/all_to_all | solution.py:137
  110.1 3.8 %while.35 = (s32[]{:T(128)}, f32[16,256]{1,0:T(8,128)S(1)}, f32[256,256]{1,0:T(8,128)S(1)}, f32[4,16,512]{2,1,0:T(8,128)S(1)}, bf16[4,512,256]{2,1,0:T(8,128)(2,...) while((s32[]{:T(128)}, f32[16,256]{1,0:T(8,128)S(1)}, f32[256,256]{1,0:T(8,128)S(1)}, ...), condition=%wide.region_11.13_spmd.clone, body=%wide.region_10.12_spmd.clone.sunk | while | flops 428220416 | bytes 1384576 | solution.py:116
  110.2 0.7 convolution_add_fusion.6
  110.9 0.2 convolution_add_fusion.5
  111.1 0.7 convolution_add_fusion.6
  111.9 0.2 convolution_add_fusion.5
  112.1 0.7 convolution_add_fusion.6
  112.8 0.2 convolution_add_fusion.5
  113.1 0.7 convolution_add_fusion.6
  114.2 0.6 dynamic_slice.49
  114.9 0.6 dynamic_slice.48
  116.2 0.7 dynamic_slice.51
  116.9 1.5 all-to-all-done
  118.6 4.0 %while.36 = (s32[]{:T(128)}, f32[256,256]{1,0:T(8,128)S(1)}, s32[2,2]{1,0:T(2,128)S(1)}, f32[2,128,128]{2,1,0:T(8,128)S(1)}, s32[]{:T(128)}) while((s32[]{:T(128)}, f32[256,256]{1,0:T(8,128)S(1)}, s32[2,2]{1,0:T(2,128)S(1)}, f32[2,128,128]{2,1,0:T(8,128)S(1)}, s32[]{:T(128)}) %tuple.98), condition=%wide.while_cond, body=%wide.while_body.sunk | while | flops 2 | bytes 131181 | solution.py:64
  118.6 0.6 fusion.64
  119.2 1.4 bitcast_dynamic-update-slice_fusion.4
  120.6 0.6 fusion.64
  121.2 1.4 bitcast_dynamic-update-slice_fusion.4
  122.6 19.9 %custom-call.23 = f32[2,128,128]{1,2,0:T(8,128)S(1)} custom-call(f32[2,128,128]{2,1,0:T(8,128)S(1)} %get-tuple-element.199), custom_call_target="InvertDiagBlocksLowerTriangular" | custom-call | tf_op jit(solution)/shard_map/while/body/eval_jaxpr/triangular_solve/custom-call.0 | solution.py:64
  142.5 0.3 fusion.24
  142.8 0.4 convolution_subtract_fusion.1
  143.2 0.3 fusion.31
  143.5 0.6 broadcast_multiply_fusion
  144.1 1.1 fusion.16
  145.4 11.7 %cholesky.49 = f32[128,128]{1,0:T(8,128)S(1)} custom-call(f32[128,128]{1,0:T(8,128)S(1)} %cholesky.115), custom_call_target="Cholesky" | custom-call | tf_op jit(solution)/shard_map/while/body/eval_jaxpr/jit(cholesky)/cholesky | solution.py:68
  157.1 9.8 %custom-call.17 = f32[1,128,128]{1,2,0:T(8,128)S(1)} custom-call(f32[1,128,128]{2,1,0:T(8,128)S(1)} %get-tuple-element.292), custom_call_target="InvertDiagBlocksLowerTriangular" | custom-call | tf_op jit(solution)/shard_map/while/body/eval_jaxpr/jit(cholesky)/cholesky | solution.py:68
  166.9 0.2 fusion.28
  167.1 0.3 convolution_subtract_fusion.2
  167.4 11.7 %cholesky.103 = f32[128,128]{1,0:T(8,128)S(1)} custom-call(f32[128,128]{1,0:T(8,128)S(1)} %convolution_subtract_fusion.2), custom_call_target="Cholesky" | custom-call | tf_op jit(solution)/shard_map/while/body/eval_jaxpr/jit(cholesky)/cholesky | solution.py:68
  179.5 0.7 compare_reduce_fusion
  180.2 0.6 compare_reduce_fusion.1
  182.3 4.3 %while.37 = (s32[]{:T(128)}, f32[256,256]{0,1:T(8,128)S(1)}, s32[2,2]{1,0:T(2,128)S(1)}, f32[2,128,128]{2,1,0:T(8,128)S(1)}, s32[]{:T(128)}) while((s32[]{:T(128)}, f32[256,256]{0,1:T(8,128)S(1)}, s32[2,2]{1,0:T(2,128)S(1)}, f32[2,128,128]{2,1,0:T(8,128)S(1)}, s32[]{:T(128)}) %tuple.110), condition=%wide.while_cond.clone, body=%wide.while_body.clone.sunk | while | flops 2 | bytes 393321 | solution.py:69
  182.3 0.6 fusion.65
  182.9 1.4 dynamic-slice.21
  184.5 0.6 fusion.65
  185.1 1.4 dynamic-slice.21
  186.6 19.9 %custom-call.24 = f32[2,128,128]{1,2,0:T(8,128)S(1)} custom-call(f32[2,128,128]{2,1,0:T(8,128)S(1)} %get-tuple-element.200), custom_call_target="InvertDiagBlocksLowerTriangular" | custom-call | tf_op jit(solution)/shard_map/while/body/eval_jaxpr/triangular_solve/custom-call.0 | solution.py:69
  206.5 0.3 fusion.22
  206.8 0.4 convolution_subtract_fusion
  207.2 0.3 fusion.27
  207.6 1.0 copy.72
  208.6 7.2 %all-to-all-start.6 = ((f32[1,1,256,256]{3,1,0,2:T(1,128)}), f32[1,1,256,256]{3,1,0,2:T(1,128)S(1)}, u32[]{:S(2)}, u32[]{:S(2)}) async-start(f32[1,1,256,256]{3,1,0,2:T(1,128)} %copy.72), calls=%async_computation.6 | async-start | bytes 524288 | tf_op jit(solution)/shard_map/all_to_all | solution.py:146
  215.8 0.5 log_add_fusion
  216.3 9.2 %all-to-all-done.6 = f32[1,1,256,256]{3,1,0,2:T(1,128)S(1)} async-done(((f32[1,1,256,256]{3,1,0,2:T(1,128)}), f32[1,1,256,256]{3,1,0,2:T(1,128)S(1)}, u32[]{:S(2)}, u32[]{:S(2)}) %all-to-all-start.6) | async-done | bytes 262176 | tf_op jit(solution)/shard_map/all_to_all | solution.py:146
  225.5 0.7 copy.79
  (71 shorter events, 2.9 us)
Async XLA Ops:
  2.6 39.1 %all-to-all-start.1 = ((bf16[16,128,256]{2,1,0:T(8,128)(2,1)}), bf16[16,128,256]{2,1,0:T(8,128)(2,1)S(1)}, u32[]{:S(2)}, u32[]{:S(2)}) async-start(bf16[16,128,256]{2,1,0:T(8,128)(2,1)} %broadcast_in_dim.32), calls=%async_computation.1 | async-start | bytes 2097152 | tf_op jit(solution)/shard_map/all_to_all | solution.py:16
  15.5 0.7 copy-start
  47.7 4.5 %copy-start.3 = (f32[16]{0:T(128)S(1)}, f32[16]{0:T(128)}, u32[]{:S(2)}) copy-start(f32[16]{0:T(128)} %param.13) | copy-start | bytes 196
  47.7 13.0 %all-to-all-start.2 = ((f32[16,16,128]{2,1,0:T(8,128)}), f32[16,16,128]{2,1,0:T(8,128)S(1)}, u32[]{:S(2)}, u32[]{:S(2)}) async-start(f32[16,16,128]{2,1,0:T(8,128)} %copy.58), calls=%async_computation.2 | async-start | bytes 262144 | tf_op jit(solution)/shard_map/all_to_all | solution.py:47
  93.1 12.6 %all-to-all-start.5 = ((f32[16,16,128]{2,1,0:T(8,128)}), f32[16,16,128]{2,1,0:T(8,128)S(1)}, u32[]{:S(2)}, u32[]{:S(2)}) async-start(f32[16,16,128]{2,1,0:T(8,128)} %broadcast_in_dim.35), calls=%async_computation.5 | async-start | bytes 262144 | tf_op jit(solution)/shard_map/all_to_all | solution.py:16
  105.7 12.7 %all-to-all-start = ((bf16[16,1,16,256]{3,2,1,0:T(8,128)(2,1)}), bf16[16,1,16,256]{3,2,1,0:T(8,128)(2,1)S(1)}, u32[]{:S(2)}, u32[]{:S(2)}) async-start(bf16[16,1,16,256]{3,2,1,0:T(8,128)(2,1)} %bitcast.4), calls=%async_computation | async-start | bytes 262144 | tf_op jit(solution)/shard_map/all_to_all | solution.py:137
  114.2 2.7 %copy-start.2 = (f32[16]{0:T(128)}, f32[16]{0:T(128)S(1)}, u32[]{:S(2)}) copy-start(f32[16]{0:T(128)S(1)} %get-tuple-element.286) | copy-start | bytes 196
  116.9 1.6 copy-start.1
  208.6 16.9 %all-to-all-start.6 = ((f32[1,1,256,256]{3,1,0,2:T(1,128)}), f32[1,1,256,256]{3,1,0,2:T(1,128)S(1)}, u32[]{:S(2)}, u32[]{:S(2)}) async-start(f32[1,1,256,256]{3,1,0,2:T(1,128)} %copy.72), calls=%async_computation.6 | async-start | bytes 524288 | tf_op jit(solution)/shard_map/all_to_all | solution.py:146
where the time goes:
time: 227 us; the launch traced here: 226 us
  other arithmetic  76.6 us (34%)
  waiting for transfers between devices  52.1 us (23%)
  starting transfers between devices  31.7 us (14%)
  blocking collectives  31.4 us (14%)
  local copies, waits for them, and re-layouts  17.9 us (8%)
  matrix products  13.1 us (6%)
  between operations  3.05 us (1%)
    another operation x7, other arithmetic, refactor(): cholesky_factor = jnp.linalg.cholesky(covariance)  34.7 us
    all_to_all x2, waiting for transfers between devices, sent_to_all(): return lax.all_to_all(copies, axis, split_axis=0, concat_axis=0, tiled=True)  32.9 us
    all_to_all x2, blocking collectives, sent_to_all(): return lax.all_to_all(copies, axis, split_axis=0, concat_axis=0, tiled=True)  31.4 us
    another operation x2, other arithmetic, refactor(): lax.linalg.triangular_solve(cholesky_factor, identity, left_side=True, lo...  19.9 us
    another operation x3, other arithmetic, refactor(): lax.linalg.triangular_solve(scaled, identity, left_side=True, lower=True)  19.9 us
    all_to_all x2, starting transfers between devices, sent_to_all(): return lax.all_to_all(copies, axis, split_axis=0, concat_axis=0, tiled=True)  15.8 us
    all_to_all x1, waiting for transfers between devices, local(): lax.all_to_all(refreshed[None], 'dp', split_axis=2, concat_axis=0, tiled=...  9.18 us
    all_to_all x1, waiting for transfers between devices, summed_on_arrival(): lax.all_to_all(tiles, axis, split_axis=0, concat_axis=0, tiled=True)  8.49 us
  transfers between devices with their start and end apart: 5, of which 5 were waited for; matrix products, arithmetic and copies ran while one was open for 4% of the time, Pallas kernels for 0%

commit v1 on v0

--- a/solution.py
+++ b/solution.py
@@ -9,6 +9,12 @@
 ridge_term = 0.01
 normal_offset = 0.9189385332046727
 exact_mode = lax.Precision.HIGHEST
+
+
+def exchange_blocks(x, axis, split, join):
+    pieces = jnp.split(x, lax.axis_size(axis), axis=split)
+    received = lax.all_to_all(jnp.stack(pieces), axis, 0, 0)
+    return jnp.concatenate(received, axis=join)
 
 
 def sent_to_all(shard, axis):
@@ -143,9 +149,9 @@
     )
     scaled = whole_factors[0].astype(jnp.float32) * lax.rsqrt(retained_own)[:, None, None]
     refreshed = lax.map(refactor, (scaled, moment_part))
-    new_factors = lax.all_to_all(
-        refreshed[None], "dp", split_axis=2, concat_axis=0, tiled=True
-    ).reshape(comp_count, row_count, features)
+    new_factors = exchange_blocks(refreshed[None], "dp", 2, 0).reshape(
+        comp_count, row_count, features
+    )
     return (new_factors, new_means, new_weights, evidence)
 
 

time: 227 us -> 236 us (1.040)
  local copies, waits for them, and re-layouts: 17.9 us -> 26.6 us
    unnamed x11 -> x26, local copies, waits for them, and re-layouts: 0.98 us -> 10.1 us
where the time goes in v1:
time: 236 us; the launch traced here: 235 us
  other arithmetic  76.6 us (32%)
  waiting for transfers between devices  52.1 us (22%)
  starting transfers between devices  31.7 us (13%)
  blocking collectives  31.4 us (13%)
  local copies, waits for them, and re-layouts  26.6 us (11%)
  matrix products  13.1 us (6%)
  between operations  3.06 us (1%)
    another operation x7, other arithmetic, refactor(): cholesky_factor = jnp.linalg.cholesky(covariance)  34.7 us
    all_to_all x2, waiting for transfers between devices, sent_to_all(): return lax.all_to_all(copies, axis, split_axis=0, concat_axis=0, tiled=True)  32.9 us
    all_to_all x2, blocking collectives, sent_to_all(): return lax.all_to_all(copies, axis, split_axis=0, concat_axis=0, tiled=True)  31.4 us
    another operation x2, other arithmetic, refactor(): lax.linalg.triangular_solve(cholesky_factor, identity, left_side=True, lo...  19.9 us
    another operation x3, other arithmetic, refactor(): lax.linalg.triangular_solve(scaled, identity, left_side=True, lower=True)  19.9 us
    all_to_all x2, starting transfers between devices, sent_to_all(): return lax.all_to_all(copies, axis, split_axis=0, concat_axis=0, tiled=True)  15.8 us
    unnamed x26, local copies, waits for them, and re-layouts  10.1 us
    all_to_all x1, waiting for transfers between devices, exchange_blocks(): received = lax.all_to_all(jnp.stack(pieces), axis, 0, 0)  9.18 us
  transfers between devices with their start and end apart: 5, of which 5 were waited for; matrix products, arithmetic and copies ran while one was open for 4% of the time, Pallas kernels for 0%

profile of v1, /device:TPU:8, one launch (start us, length us, event | category | flops | bytes accessed | tf_op | source)
XLA Modules:
  0.0 234.9 jit_solution(7811785068693116390)
XLA Ops:
  0.6 1.9 broadcast_in_dim.32
  2.6 11.8 %all-to-all-start.1 = ((bf16[16,128,256]{2,1,0:T(8,128)(2,1)}), bf16[16,128,256]{2,1,0:T(8,128)(2,1)S(1)}, u32[]{:S(2)}, u32[]{:S(2)}) async-start(bf16[16,128,256]{2,1,0:T(8,128)(2,1)} %broadcast_in_dim.32), calls=%async_computation.1 | async-start | bytes 2097152 | tf_op jit(solution)/shard_map/all_to_all | solution.py:22
  14.4 0.9 constant_dynamic-slice_fusion.5
  15.5 0.6 gather_fusion
  16.2 1.1 fusion.33
  17.3 24.4 %all-to-all-done.1 = bf16[16,128,256]{2,1,0:T(8,128)(2,1)S(1)} async-done(((bf16[16,128,256]{2,1,0:T(8,128)(2,1)}), bf16[16,128,256]{2,1,0:T(8,128)(2,1)S(1)}, u32[]{:S(2)}, u32[]{:S(2)}) %all-to-all-start.1) | async-done | bytes 1048608 | tf_op jit(solution)/shard_map/all_to_all | solution.py:22
  41.7 5.2 %while.34 = (s32[]{:T(128)}, f32[4,16,512]{2,1,0:T(8,128)S(1)}, f32[16]{0:T(128)S(1)}, bf16[4,512,256]{2,1,0:T(8,128)(2,1)S(1)}, bf16[256,256]{1,0:T(8,128)(2,1)}, /*index=5*/f32[16,16]{1,0:T(8,128)S(1)}, s32[]{:T(128)}) while((s32[]{:T(128)}, f32[4,16,512]{2,1,0:T(8,128)S(1)}, f32[16]{0:T(128)S(1)}, bf16[4,512,256]{2,1,0:T(8,128)(2,1)S(1)}, ...), condition=%wide.region_3.4_spmd, body=%wide.region_1.3_spmd.sunk | while | flops 67510272 | bytes 500309 | solution.py:102
  41.7 1.2 multiply_reduce_fusion.2
  43.0 1.2 multiply_reduce_fusion.2
  44.3 1.2 multiply_reduce_fusion.2
  45.6 1.2 multiply_reduce_fusion.2
  47.0 0.7 copy.56
  47.7 4.5 %all-to-all-start.2 = ((f32[16,16,128]{2,1,0:T(8,128)}), f32[16,16,128]{2,1,0:T(8,128)S(1)}, u32[]{:S(2)}, u32[]{:S(2)}) async-start(f32[16,16,128]{2,1,0:T(8,128)} %copy.56), calls=%async_computation.2 | async-start | bytes 262144 | tf_op jit(solution)/shard_map/all_to_all | solution.py:53
  52.2 8.5 %all-to-all-done.2 = f32[16,16,128]{2,1,0:T(8,128)S(1)} async-done(((f32[16,16,128]{2,1,0:T(8,128)}), f32[16,16,128]{2,1,0:T(8,128)S(1)}, u32[]{:S(2)}, u32[]{:S(2)}) %all-to-all-start.2) | async-done | bytes 131104 | tf_op jit(solution)/shard_map/all_to_all | solution.py:53
  60.8 18.6 %all_to_all.41 = f32[32,1,128]{2,1,0:T(1,128)S(1)} all-to-all(f32[32,1,128]{2,1,0:T(1,128)S(1)} %broadcast_in_dim.33), channel_id=1, replica_groups=mesh['dp'=16,'comp'=32] {'comp'}, dimensions={0} | all-to-all | bytes 32768 | tf_op jit(solution)/shard_map/all_to_all | solution.py:22
  79.6 12.8 %all_to_all.42 = f32[32,1,128]{2,1,0:T(1,128)S(1)} all-to-all(f32[32,1,128]{2,1,0:T(1,128)S(1)} %broadcast_in_dim.34), channel_id=1, replica_groups=mesh['dp'=16,'comp'=32] {'comp'}, dimensions={0} | all-to-all | bytes 32768 | tf_op jit(solution)/shard_map/all_to_all | solution.py:22
  92.4 0.7 broadcast_in_dim.35
  93.1 4.0 %all-to-all-start.5 = ((f32[16,16,128]{2,1,0:T(8,128)}), f32[16,16,128]{2,1,0:T(8,128)S(1)}, u32[]{:S(2)}, u32[]{:S(2)}) async-start(f32[16,16,128]{2,1,0:T(8,128)} %broadcast_in_dim.35), calls=%async_computation.5 | async-start | bytes 262144 | tf_op jit(solution)/shard_map/all_to_all | solution.py:22
  97.2 8.5 %all-to-all-done.5 = f32[16,16,128]{2,1,0:T(8,128)S(1)} async-done(((f32[16,16,128]{2,1,0:T(8,128)}), f32[16,16,128]{2,1,0:T(8,128)S(1)}, u32[]{:S(2)}, u32[]{:S(2)}) %all-to-all-start.5) | async-done | bytes 131104 | tf_op jit(solution)/shard_map/all_to_all | solution.py:22
  105.7 4.3 %all-to-all-start = ((bf16[16,1,16,256]{3,2,1,0:T(8,128)(2,1)}), bf16[16,1,16,256]{3,2,1,0:T(8,128)(2,1)S(1)}, u32[]{:S(2)}, u32[]{:S(2)}) async-start(bf16[16,1,16,256]{3,2,1,0:T(8,128)(2,1)} %bitcast.4), calls=%async_computation | async-start | bytes 262144 | tf_op jit(solution)/shard_map/all_to_all | solution.py:143
  110.1 3.8 %while.35 = (s32[]{:T(128)}, f32[16,256]{1,0:T(8,128)S(1)}, f32[256,256]{1,0:T(8,128)S(1)}, f32[4,16,512]{2,1,0:T(8,128)S(1)}, bf16[4,512,256]{2,1,0:T(8,128)(2,...) while((s32[]{:T(128)}, f32[16,256]{1,0:T(8,128)S(1)}, f32[256,256]{1,0:T(8,128)S(1)}, ...), condition=%wide.region_11.13_spmd.clone, body=%wide.region_10.12_spmd.clone.sunk | while | flops 428220416 | bytes 1384576 | solution.py:122
  110.2 0.7 convolution_add_fusion.6
  111.1 0.7 convolution_add_fusion.6
  112.1 0.7 convolution_add_fusion.6
  113.1 0.7 convolution_add_fusion.6
  114.9 0.6 dynamic_slice.48
  116.2 0.7 dynamic_slice.51
  116.9 1.5 all-to-all-done
  118.6 4.0 %while.36 = (s32[]{:T(128)}, f32[256,256]{1,0:T(8,128)S(1)}, s32[2,2]{1,0:T(2,128)S(1)}, f32[2,128,128]{2,1,0:T(8,128)S(1)}, s32[]{:T(128)}) while((s32[]{:T(128)}, f32[256,256]{1,0:T(8,128)S(1)}, s32[2,2]{1,0:T(2,128)S(1)}, f32[2,128,128]{2,1,0:T(8,128)S(1)}, s32[]{:T(128)}) %tuple.98), condition=%wide.while_cond, body=%wide.while_body.sunk | while | flops 2 | bytes 131181 | solution.py:70
  118.6 0.6 fusion.64
  119.2 1.4 bitcast_dynamic-update-slice_fusion.4
  121.2 1.4 bitcast_dynamic-update-slice_fusion.4
  122.6 19.9 %custom-call.23 = f32[2,128,128]{1,2,0:T(8,128)S(1)} custom-call(f32[2,128,128]{2,1,0:T(8,128)S(1)} %get-tuple-element.199), custom_call_target="InvertDiagBlocksLowerTriangular" | custom-call | tf_op jit(solution)/shard_map/while/body/eval_jaxpr/triangular_solve/custom-call.0 | solution.py:70
  144.1 1.1 fusion.16
  145.4 11.7 %cholesky.49 = f32[128,128]{1,0:T(8,128)S(1)} custom-call(f32[128,128]{1,0:T(8,128)S(1)} %cholesky.115), custom_call_target="Cholesky" | custom-call | tf_op jit(solution)/shard_map/while/body/eval_jaxpr/jit(cholesky)/cholesky | solution.py:74
  157.1 9.8 %custom-call.17 = f32[1,128,128]{1,2,0:T(8,128)S(1)} custom-call(f32[1,128,128]{2,1,0:T(8,128)S(1)} %get-tuple-element.292), custom_call_target="InvertDiagBlocksLowerTriangular" | custom-call | tf_op jit(solution)/shard_map/while/body/eval_jaxpr/jit(cholesky)/cholesky | solution.py:74
  167.4 11.7 %cholesky.103 = f32[128,128]{1,0:T(8,128)S(1)} custom-call(f32[128,128]{1,0:T(8,128)S(1)} %convolution_subtract_fusion.2), custom_call_target="Cholesky" | custom-call | tf_op jit(solution)/shard_map/while/body/eval_jaxpr/jit(cholesky)/cholesky | solution.py:74
  179.5 0.7 compare_reduce_fusion
  180.2 0.6 compare_reduce_fusion.1
  182.3 4.3 %while.37 = (s32[]{:T(128)}, f32[256,256]{0,1:T(8,128)S(1)}, s32[2,2]{1,0:T(2,128)S(1)}, f32[2,128,128]{2,1,0:T(8,128)S(1)}, s32[]{:T(128)}) while((s32[]{:T(128)}, f32[256,256]{0,1:T(8,128)S(1)}, s32[2,2]{1,0:T(2,128)S(1)}, f32[2,128,128]{2,1,0:T(8,128)S(1)}, s32[]{:T(128)}) %tuple.112), condition=%wide.while_cond.clone, body=%wide.while_body.clone.sunk | while | flops 2 | bytes 393321 | solution.py:75
  182.3 0.6 fusion.65
  182.9 1.4 dynamic-slice.21
  184.5 0.6 fusion.65
  185.1 1.4 dynamic-slice.21
  186.6 19.9 %custom-call.24 = f32[2,128,128]{1,2,0:T(8,128)S(1)} custom-call(f32[2,128,128]{2,1,0:T(8,128)S(1)} %get-tuple-element.200), custom_call_target="InvertDiagBlocksLowerTriangular" | custom-call | tf_op jit(solution)/shard_map/while/body/eval_jaxpr/triangular_solve/custom-call.0 | solution.py:75
  207.6 0.6 constant_dynamic-update-slice_fusion.15
  208.2 0.6 constant_dynamic-update-slice_fusion.14
  208.8 0.6 constant_dynamic-update-slice_fusion.13
  209.4 0.6 constant_dynamic-update-slice_fusion.12
  210.0 0.6 constant_dynamic-update-slice_fusion.11
  210.6 0.6 constant_dynamic-update-slice_fusion.10
  211.2 0.6 constant_dynamic-update-slice_fusion.9
  211.8 0.6 constant_dynamic-update-slice_fusion.8
  212.4 0.6 constant_dynamic-update-slice_fusion.7
  213.1 0.6 constant_dynamic-update-slice_fusion.6
  213.7 0.6 constant_dynamic-update-slice_fusion.5
  214.3 0.6 constant_dynamic-update-slice_fusion.4
  214.9 0.6 constant_dynamic-update-slice_fusion.3
  215.5 0.6 constant_dynamic-update-slice_fusion.2
  216.1 0.6 constant_dynamic-update-slice_fusion.1
  216.7 0.6 constant_dynamic-update-slice_fusion
  217.3 7.2 %all-to-all-start.6 = ((f32[16,1,1,16,256]{4,3,2,1,0:T(8,128)}), f32[16,1,1,16,256]{4,3,2,1,0:T(8,128)S(1)}, u32[]{:S(2)}, u32[]{:S(2)}) async-start(f32[16,1,1,16,256]{4,3,2,1,0:T(8,128)} %constant_dynamic-update-slice_fusion), calls=%async_computation.6 | async-start | bytes 524288 | tf_op jit(solution)/shard_map/all_to_all | solution.py:16
  225.0 9.2 %all-to-all-done.6 = f32[16,1,1,16,256]{4,3,2,1,0:T(8,128)S(1)} async-done(((f32[16,1,1,16,256]{4,3,2,1,0:T(8,128)}), f32[16,1,1,16,256]{4,3,2,1,0:T(8,128)S(1)}, u32[]{:S(2)}, u32[]{:S(2)}) %all-to-all-start.6) | async-done | bytes 262176 | tf_op jit(solution)/shard_map/all_to_all | solution.py:16
  234.2 0.7 copy.135
  (86 shorter events, 8.2 us)
Async XLA Ops:
  2.6 39.1 %all-to-all-start.1 = ((bf16[16,128,256]{2,1,0:T(8,128)(2,1)}), bf16[16,128,256]{2,1,0:T(8,128)(2,1)S(1)}, u32[]{:S(2)}, u32[]{:S(2)}) async-start(bf16[16,128,256]{2,1,0:T(8,128)(2,1)} %broadcast_in_dim.32), calls=%async_computation.1 | async-start | bytes 2097152 | tf_op jit(solution)/shard_map/all_to_all | solution.py:22
  15.5 0.7 copy-start
  47.7 4.5 %copy-start.3 = (f32[16]{0:T(128)S(1)}, f32[16]{0:T(128)}, u32[]{:S(2)}) copy-start(f32[16]{0:T(128)} %param.13) | copy-start | bytes 196
  47.7 13.0 %all-to-all-start.2 = ((f32[16,16,128]{2,1,0:T(8,128)}), f32[16,16,128]{2,1,0:T(8,128)S(1)}, u32[]{:S(2)}, u32[]{:S(2)}) async-start(f32[16,16,128]{2,1,0:T(8,128)} %copy.56), calls=%async_computation.2 | async-start | bytes 262144 | tf_op jit(solution)/shard_map/all_to_all | solution.py:53
  93.1 12.6 %all-to-all-start.5 = ((f32[16,16,128]{2,1,0:T(8,128)}), f32[16,16,128]{2,1,0:T(8,128)S(1)}, u32[]{:S(2)}, u32[]{:S(2)}) async-start(f32[16,16,128]{2,1,0:T(8,128)} %broadcast_in_dim.35), calls=%async_computation.5 | async-start | bytes 262144 | tf_op jit(solution)/shard_map/all_to_all | solution.py:22
  105.7 12.7 %all-to-all-start = ((bf16[16,1,16,256]{3,2,1,0:T(8,128)(2,1)}), bf16[16,1,16,256]{3,2,1,0:T(8,128)(2,1)S(1)}, u32[]{:S(2)}, u32[]{:S(2)}) async-start(bf16[16,1,16,256]{3,2,1,0:T(8,128)(2,1)} %bitcast.4), calls=%async_computation | async-start | bytes 262144 | tf_op jit(solution)/shard_map/all_to_all | solution.py:143
  114.2 2.7 %copy-start.2 = (f32[16]{0:T(128)}, f32[16]{0:T(128)S(1)}, u32[]{:S(2)}) copy-start(f32[16]{0:T(128)S(1)} %get-tuple-element.512) | copy-start | bytes 196
  116.9 1.6 copy-start.1
  217.3 16.9 %all-to-all-start.6 = ((f32[16,1,1,16,256]{4,3,2,1,0:T(8,128)}), f32[16,1,1,16,256]{4,3,2,1,0:T(8,128)S(1)}, u32[]{:S(2)}, u32[]{:S(2)}) async-start(f32[16,1,1,16,256]{4,3,2,1,0:T(8,128)} %constant_dynamic-update-slice_fusion), calls=%async_computation.6 | async-start | bytes 524288 | tf_op jit(solution)/shard_map/all_to_all | solution.py:16
